TPU v7x, 32 devices: a whole 2x2x4 slice. The times are simulated.
32 devices in a mesh: batch: 16 (over z, y, x), strip: 2 (over core).
Axes of the slice: x: 2, y: 2, z: 4, core: 2. Of those that a mesh axis runs over, the one named last changes fastest.
Arguments:
- state_maps: bfloat16 [16, 32, 64, 256], P('batch', 'strip'), may hold values from -6 to 6
- goal_maps: bfloat16 [16, 32, 64, 256], P('batch', 'strip'), may hold values from -6 to 6
- conv_one: bfloat16 [3, 3, 256, 256], replicated, may hold values from -0.125 to 0.125
- conv_two: bfloat16 [3, 3, 256, 256], replicated, may hold values from -0.125 to 0.125
- state_proj: bfloat16 [256, 1024], replicated, may hold values from -0.375 to 0.375
- goal_proj: bfloat16 [256, 1024], replicated, may hold values from -0.375 to 0.375
- inv_temp: float32 [1], replicated, may hold values from 4 to 16
- pair_index: int32 [16], P('batch'), may hold values from 0 to 15, each once
Outputs:
- pair_loss: float32 [16], P('batch')
- grad_state_proj: float32 [256, 1024], replicated
- grad_goal_proj: float32 [256, 1024], replicated
- block_maps: float32 [2, 16, 32, 64, 256], P(None, 'batch', 'strip')
Inputs may be any that keep to these rules, and one draw needn't show every extreme that they name: pair_index names each goal of 0 to 15 exactly once.
All inputs are finite; a program needn't handle non-finite values.
Results may differ from a plain program's by a relative error of at most 0.017.
Values may be sent and summed in bfloat16 or wider, within the bound.
A program may use at most 64 MiB of HBM per device.

v0:
```python
import functools

import jax
import jax.numpy as jnp
from jax import lax
from jax.experimental import pallas as pl
from jax.experimental.pallas import tpu as pltpu
from jax.sharding import PartitionSpec as P

MESH = pl.DeviceIdType.MESH
BF = jnp.bfloat16
F32 = jnp.float32
LANES = 128
ROWS_AT_ONCE = 6


def spread(dst, frame, row, cells):
    rows, columns, channels = cells.shape
    where = lax.broadcasted_iota(jnp.int32, cells.shape, 1)
    left = jnp.where(where == 0, 0.0, pltpu.roll(cells, 1, axis=1))
    right = jnp.where(where == columns - 1, 0.0, pltpu.roll(cells, columns - 1, axis=1))
    span = pl.ds(row, rows)
    dst[frame, span, :, 0:channels] = left.astype(BF)
    dst[frame, span, :, channels : 2 * channels] = cells.astype(BF)
    dst[frame, span, :, 2 * channels : 3 * channels] = right.astype(BF)


def chunks(start, stop):
    number = -(-(stop - start) // ROWS_AT_ONCE)
    cuts = [start + (stop - start) * i // number for i in range(number + 1)]
    return [(low, high - low) for low, high in zip(cuts, cuts[1:])]


def taps(src, frame, row, rows):
    columns, width = src.shape[2], src.shape[3]
    return jnp.concatenate(
        [src[frame, row + d : row + d + rows].reshape(rows * columns, width) for d in range(3)],
        axis=1,
    )


def block_kernel(
    batches, strips,
    state_ref, goal_ref, one_ref, two_ref, sproj_ref, gproj_ref, index_ref,
    block_ref, gathered_ref, marks_out, sproj_out, gproj_out,
    maps, wide_one, wide_two, w_one, w_two, halo, mark, marks, part, parts, note, notes,
    load_sem, halo_send, halo_recv,
    mark_send, mark_recv, part_send, part_recv, note_send, note_recv,
):
    b = lax.axis_index("batch")
    s = lax.axis_index("strip")
    rows, columns, channels = maps.shape[1], maps.shape[2], maps.shape[3]
    packs = channels // LANES

    loads = [
        pltpu.make_async_copy(source, target, load_sem.at[i])
        for i, (source, target) in enumerate((
            (state_ref.at[0], maps.at[0]),
            (goal_ref.at[0], maps.at[1]),
            (one_ref, w_one),
            (two_ref, w_two),
            (sproj_ref, sproj_out),
            (gproj_ref, gproj_out),
        ))
    ]
    for copy in loads:
        copy.start()

    @pl.when(s == 0)
    def _():
        halo[0] = jnp.zeros(halo.shape[1:], BF)

    @pl.when(s == strips - 1)
    def _():
        halo[1] = jnp.zeros(halo.shape[1:], BF)

    barrier = pltpu.get_barrier_semaphore()

    def greet_strip(k, carry):
        pl.semaphore_signal(barrier, inc=1, device_id=(b, lax.rem(s + k, strips)), device_id_type=MESH)
        return carry

    def greet_batch(k, carry):
        pl.semaphore_signal(barrier, inc=1, device_id=(lax.rem(b + k, batches), s), device_id_type=MESH)
        return carry

    lax.fori_loop(1, batches, greet_batch, 0)
    lax.fori_loop(1, strips, greet_strip, 0)

    def part_copy(k):
        return pltpu.make_async_remote_copy(
            src_ref=part, dst_ref=parts.at[s],
            send_sem=part_send.at[k], recv_sem=part_recv.at[k],
            device_id=(b, lax.rem(s + k, strips)), device_id_type=MESH,
        )

    def note_copy(k):
        return pltpu.make_async_remote_copy(
            src_ref=note, dst_ref=notes.at[b],
            send_sem=note_send.at[k], recv_sem=note_recv.at[k],
            device_id=(lax.rem(b + k, batches), s), device_id_type=MESH,
        )

    def mark_copy(k):
        return pltpu.make_async_remote_copy(
            src_ref=mark, dst_ref=marks.at[b],
            send_sem=mark_send.at[k], recv_sem=mark_recv.at[k],
            device_id=(lax.rem(b + k, batches), s), device_id_type=MESH,
        )

    def start(make, count):
        def one(k, carry):
            make(k).start()
            return carry

        lax.fori_loop(1, count, one, 0)

    def finish(make, count):
        def one(k, carry):
            make(k).wait()
            return carry

        lax.fori_loop(1, count, one, 0)

    loads[0].wait()
    spread(wide_one, 0, 2, jnp.maximum(maps[0].astype(F32), 0.0))
    told = jnp.full(mark.shape, index_ref[0].astype(F32))
    mark[...] = told
    marks[b] = told
    loads[1].wait()
    pl.semaphore_wait(barrier, strips + batches - 2)
    down = pltpu.make_async_remote_copy(
        src_ref=maps.at[:, rows - 2 : rows], dst_ref=halo.at[0],
        send_sem=halo_send.at[0], recv_sem=halo_recv.at[0],
        device_id=(b, lax.rem(s + 1, strips)), device_id_type=MESH,
    )
    up = pltpu.make_async_remote_copy(
        src_ref=maps.at[:, 0:2], dst_ref=halo.at[1],
        send_sem=halo_send.at[1], recv_sem=halo_recv.at[1],
        device_id=(b, lax.rem(s + strips - 1, strips)), device_id_type=MESH,
    )

    @pl.when(s < strips - 1)
    def _():
        down.start()

    @pl.when(s > 0)
    def _():
        up.start()

    start(mark_copy, batches)

    above = jnp.where(s > 0, 1.0, 0.0)
    below = jnp.where(s < strips - 1, 1.0, 0.0)

    def first(pieces):
        lhs = [taps(wide_one, f, r + 1, count) for f, r, count in pieces]
        lhs = lhs[0] if len(lhs) == 1 else jnp.concatenate(lhs, axis=0)
        out = jnp.maximum(jnp.dot(lhs, w_one[...], preferred_element_type=F32), 0.0)
        at = 0
        for f, r, count in pieces:
            piece = out[at : at + count * columns].reshape(count, columns, channels)
            at += count * columns
            if r < 0:
                piece = jnp.concatenate([piece[0:1] * above, piece[1:]], axis=0)
            if r + count > rows:
                piece = jnp.concatenate([piece[: count - 1], piece[count - 1 :] * below], axis=0)
            spread(wide_two, f, r + 1, piece)

    spread(wide_one, 1, 2, jnp.maximum(maps[1].astype(F32), 0.0))
    loads[2].wait()
    for r, count in chunks(1, rows - 1):
        first([(0, r, count)])

    loads[3].wait()

    @pl.when(s < strips - 1)
    def _():
        down.wait_send()
        up.wait_recv()

    @pl.when(s > 0)
    def _():
        up.wait_send()
        down.wait_recv()

    for f in range(2):
        spread(wide_one, f, 0, jnp.maximum(halo[0, f].astype(F32), 0.0))
        spread(wide_one, f, rows + 2, jnp.maximum(halo[1, f].astype(F32), 0.0))
    first([(0, -1, 2), (0, rows - 1, 2)])
    for r, count in chunks(-1, rows + 1):
        first([(1, r, count)])
    sums = []
    for f in range(2):
        total = jnp.zeros((1, channels), F32)
        for r, count in chunks(0, rows):
            skip = maps[f, r : r + count].reshape(count * columns, channels).astype(F32)
            out = jnp.dot(taps(wide_two, f, r, count), w_two[...], preferred_element_type=F32)
            out = jnp.maximum(skip + out, 0.0)
            block_ref[f, 0, r : r + count] = out.reshape(count, columns, channels)
            total = total + jnp.sum(out, axis=0, keepdims=True)
        sums.append(total)

    cells = rows * strips * columns
    lines = [total[:, LANES * p : LANES * (p + 1)] / cells for total in sums for p in range(packs)]
    share = jnp.concatenate(lines, axis=0)
    part[...] = share
    parts[s] = share
    start(part_copy, strips)
    finish(part_copy, strips)
    pooled = jnp.sum(parts[...], axis=0).astype(BF)
    note[...] = pooled
    notes[b] = pooled
    start(note_copy, batches)
    finish(mark_copy, batches)
    marks_out[...] = jnp.concatenate([marks[i, 0:1] for i in range(batches)], axis=0)
    finish(note_copy, batches)
    gathered_ref[...] = notes[...]
    loads[4].wait()
    loads[5].wait()


def unit_of(emb):
    inverse = lax.rsqrt(jnp.sum(emb * emb, axis=-1, keepdims=True) + 1e-06)
    return emb * inverse, inverse


def dot(left, right, over):
    return lax.dot_general(left, right, ((over[0:1], over[1:2]), ((), ())), preferred_element_type=F32)


def head_kernel(
    block_ref, gathered_ref, marks_ref, sproj_ref, gproj_ref, temp_ref,
    loss_ref, sgrad_ref, ggrad_ref, out_ref,
    loss, sgrad, ggrad, sem,
):
    keep = pltpu.make_async_copy(block_ref, out_ref, sem.at[0])
    keep.start()
    batches = gathered_ref.shape[0]
    packs = sproj_ref.shape[0] // LANES
    heard = gathered_ref[...].astype(F32)

    def column(p):
        return jnp.concatenate([heard[i, p : p + 1] for i in range(batches)], axis=0)

    state_pool = jnp.concatenate([column(p) for p in range(packs)], axis=1).astype(BF)
    goal_pool = jnp.concatenate([column(packs + p) for p in range(packs)], axis=1).astype(BF)
    index = marks_ref[:, 0:batches]
    sharpness = temp_ref[0]
    state_unit, state_inverse = unit_of(dot(state_pool, sproj_ref[...], (1, 0)))
    goal_unit, goal_inverse = unit_of(dot(goal_pool, gproj_ref[...], (1, 0)))
    state_bf = state_unit.astype(BF)
    goal_bf = goal_unit.astype(BF)
    logits = sharpness * dot(state_bf, goal_bf, (1, 1))
    exp_logits = jnp.exp(logits)
    row_total = jnp.sum(exp_logits, axis=1, keepdims=True)
    matched = lax.broadcasted_iota(jnp.int32, logits.shape, 1).astype(F32) == index
    positive = jnp.sum(jnp.where(matched, logits, 0.0), axis=1, keepdims=True)
    losses = jnp.log(row_total) - positive
    mine = lax.broadcasted_iota(jnp.int32, losses.shape, 0) == lax.axis_index("batch")
    loss[0] = jnp.sum(jnp.where(mine, losses, 0.0))
    say = pltpu.make_async_copy(loss, loss_ref, sem.at[1])
    say.start()
    logit_grad = (exp_logits / row_total - matched.astype(F32)).astype(BF)
    copies = [keep, say]
    for pool, unit, inverse, unit_grad, grad, target in (
        (state_pool, state_unit, state_inverse, dot(logit_grad, goal_bf, (1, 0)), sgrad, sgrad_ref),
        (goal_pool, goal_unit, goal_inverse, dot(logit_grad, state_bf, (0, 0)), ggrad, ggrad_ref),
    ):
        unit_grad = sharpness * unit_grad
        along = jnp.sum(unit * unit_grad, axis=-1, keepdims=True)
        emb_grad = ((unit_grad - unit * along) * inverse).astype(BF)
        for p in range(packs):
            span = slice(LANES * p, LANES * (p + 1))
            grad[span] = dot(pool[:, span], emb_grad, (0, 0))
            copies.append(pltpu.make_async_copy(grad.at[span], target.at[span], sem.at[len(copies)]))
            copies[-1].start()
    for copy in copies:
        copy.wait()


def shards(batches, strips, state_maps, goal_maps, conv_one, conv_two, state_proj, goal_proj, inv_temp, pair_index):
    _, rows, columns, channels = state_maps.shape
    width = state_proj.shape[1]
    taps_in = conv_one.shape[0] * conv_one.shape[1] * channels
    any_spec = pl.BlockSpec(memory_space=pl.ANY)
    smem = pl.BlockSpec(memory_space=pltpu.SMEM)
    vmem = pl.BlockSpec(memory_space=pltpu.VMEM)
    block_shape = (2, 1, rows, columns, channels)
    dma = pltpu.SemaphoreType.DMA
    lines = 2 * channels // LANES
    stay = [
        pltpu.with_memory_space_constraint(value, pltpu.HBM)
        for value in (
            state_maps, goal_maps,
            conv_one.reshape(taps_in, channels), conv_two.reshape(taps_in, channels),
            state_proj, goal_proj,
        )
    ]
    held = pl.pallas_call(
        functools.partial(block_kernel, batches, strips),
        out_shape=(
            pltpu.VMEM(block_shape, F32),
            pltpu.VMEM((batches, lines, LANES), BF),
            pltpu.VMEM((batches, LANES), F32),
            pltpu.VMEM((channels, width), BF),
            pltpu.VMEM((channels, width), BF),
        ),
        in_specs=[any_spec] * 6 + [smem],
        out_specs=(vmem,) * 5,
        scratch_shapes=[
            pltpu.VMEM((2, rows, columns, channels), BF),
            pltpu.VMEM((2, rows + 4, columns, 3 * channels), BF),
            pltpu.VMEM((2, rows + 2, columns, 3 * channels), BF),
            pltpu.VMEM((taps_in, channels), BF),
            pltpu.VMEM((taps_in, channels), BF),
            pltpu.VMEM((2, 2, 2, columns, channels), BF),
            pltpu.VMEM((8, LANES), F32),
            pltpu.VMEM((batches, 8, LANES), F32),
            pltpu.VMEM((lines, LANES), F32),
            pltpu.VMEM((strips, lines, LANES), F32),
            pltpu.VMEM((lines, LANES), BF),
            pltpu.VMEM((batches, lines, LANES), BF),
            dma((6,)), dma((2,)), dma((2,)), dma((batches,)), dma((batches,)),
            dma((strips,)), dma((strips,)), dma((batches,)), dma((batches,)),
        ],
        compiler_params=pltpu.CompilerParams(
            collective_id=0, has_side_effects=True, vmem_limit_bytes=40 * 2**20
        ),
        name="block",
    )(*stay, pair_index)
    held = [pltpu.with_memory_space_constraint(value, pltpu.VMEM) for value in held]
    return pl.pallas_call(
        head_kernel,
        out_shape=(
            jax.ShapeDtypeStruct((1,), F32),
            jax.ShapeDtypeStruct((channels, width), F32),
            jax.ShapeDtypeStruct((channels, width), F32),
            jax.ShapeDtypeStruct(block_shape, F32),
        ),
        in_specs=[vmem] * 5 + [smem],
        out_specs=(any_spec,) * 4,
        scratch_shapes=[
            pltpu.SMEM((1,), F32),
            pltpu.VMEM((channels, width), F32),
            pltpu.VMEM((channels, width), F32),
            dma((2 + 2 * (channels // LANES),)),
        ],
        compiler_params=pltpu.CompilerParams(vmem_limit_bytes=40 * 2**20),
        name="head",
    )(*held, inv_temp)


def solution(mesh):
    placed = (
        P("batch", "strip", None, None),
        P("batch", "strip", None, None),
        P(),
        P(),
        P(),
        P(),
        P(),
        P("batch"),
    )
    return jax.shard_map(
        functools.partial(shards, mesh.shape["batch"], mesh.shape["strip"]),
        mesh=mesh,
        in_specs=placed,
        out_specs=(P("batch"), P(), P(), P(None, "batch", "strip", None, None)),
        check_vma=False,
    )
```

profile of v0, /device:TPU:0, one launch (start us, length us, event | category | flops | bytes accessed | tf_op | source)
XLA Modules:
  0.0 22.4 jit_solution(5754709563438857209)
XLA Ops:
  1.9 18.1 %block.1 = (f32[2,1,16,64,256]{4,3,2,1,0:T(8,128)S(1)}, bf16[16,4,128]{2,1,0:T(4,128)(2,1)S(1)}, f32[16,128]{1,0:T(8,128)S(1)}, bf16[256,1024]{1,0:T(8,128)(2,1)S(1)}, bf16[256,1024]{1,0:T(8,128)(2,1)S(1)}) custom-call(bf16[1,16,64,256]{3,2,1,0:T(8,128)(2,1)} %state_ref.1, bf16[1,16,64,256]{3,2,1,0:T(8,128)(2,1)} %goal_ref.1, bf16[2304,256]{1,0:T(8,128)(2,1)} %bitcast.2, ...), custom_call_target="tpu_custom_call" | custom-call | tf_op jit(solution)/shard_map/block/pallas_call | solution.py:300
  20.0 2.4 %head.1 = (f32[1]{0:T(128)}, f32[256,1024]{1,0:T(8,128)}, f32[256,1024]{1,0:T(8,128)}, f32[2,1,16,64,256]{4,3,2,1,0:T(8,128)}) custom-call(f32[2,1,16,64,256]{4,3,2,1,0:T(8,128)S(1)} %get-tuple-element.9.block_ref, bf16[16,4,128]{2,1,0:T(4,128)(2,1)S(1)} %get-tuple-element.10.gathered_ref, f32[16,128]{1,0:T(8,128)S(1)} %get-tuple-element.11.marks_ref, ...), custom_call_target="tpu_custom_call" | custom-call | tf_op jit(solution)/shard_map/head/pallas_call | solution.py:333
where the time goes:
time: 22.5 us; the launch traced here: 22.4 us
  Pallas kernels  20.4 us (91%)
  between operations  1.93 us (9%)
    pallas_call x1, Pallas kernels, shards(): pl.pallas_call(functools.partial(block_kernel, batches, strips), out_shap...  18.1 us
    pallas_call x1, Pallas kernels, shards(): pl.pallas_call(head_kernel, out_shape=(jax.ShapeDtypeStruct((1,), F32), j...  2.37 us

commit v1 on v0

--- a/solution.py
+++ b/solution.py
@@ -41,16 +41,17 @@
 
 def block_kernel(
     batches, strips,
-    state_ref, goal_ref, one_ref, two_ref, sproj_ref, gproj_ref, index_ref,
-    block_ref, gathered_ref, marks_out, sproj_out, gproj_out,
-    maps, wide_one, wide_two, w_one, w_two, halo, mark, marks, part, parts, note, notes,
-    load_sem, halo_send, halo_recv,
-    mark_send, mark_recv, part_send, part_recv, note_send, note_recv,
+    state_ref, goal_ref, one_ref, two_ref, sproj_ref, gproj_ref, index_ref, temp_ref,
+    block_ref, gathered_ref, sproj_out, gproj_out,
+    maps, wide_one, wide_two, w_one, w_two, halo, index, temp, part, parts,
+    load_sem, halo_send, halo_recv, part_send, part_recv,
 ):
     b = lax.axis_index("batch")
     s = lax.axis_index("strip")
     rows, columns, channels = maps.shape[1], maps.shape[2], maps.shape[3]
     packs = channels // LANES
+    devices = batches * strips
+    me = b * strips + s
 
     loads = [
         pltpu.make_async_copy(source, target, load_sem.at[i])
@@ -61,6 +62,8 @@
             (two_ref, w_two),
             (sproj_ref, sproj_out),
             (gproj_ref, gproj_out),
+            (index_ref, index),
+            (temp_ref, temp),
         ))
     ]
     for copy in loads:
@@ -76,59 +79,19 @@
 
     barrier = pltpu.get_barrier_semaphore()
 
-    def greet_strip(k, carry):
-        pl.semaphore_signal(barrier, inc=1, device_id=(b, lax.rem(s + k, strips)), device_id_type=MESH)
+    def greet(k, carry):
+        other = lax.rem(me + k, devices)
+        pl.semaphore_signal(
+            barrier, inc=1, device_id=(other // strips, lax.rem(other, strips)), device_id_type=MESH
+        )
         return carry
 
-    def greet_batch(k, carry):
-        pl.semaphore_signal(barrier, inc=1, device_id=(lax.rem(b + k, batches), s), device_id_type=MESH)
-        return carry
-
-    lax.fori_loop(1, batches, greet_batch, 0)
-    lax.fori_loop(1, strips, greet_strip, 0)
-
-    def part_copy(k):
-        return pltpu.make_async_remote_copy(
-            src_ref=part, dst_ref=parts.at[s],
-            send_sem=part_send.at[k], recv_sem=part_recv.at[k],
-            device_id=(b, lax.rem(s + k, strips)), device_id_type=MESH,
-        )
-
-    def note_copy(k):
-        return pltpu.make_async_remote_copy(
-            src_ref=note, dst_ref=notes.at[b],
-            send_sem=note_send.at[k], recv_sem=note_recv.at[k],
-            device_id=(lax.rem(b + k, batches), s), device_id_type=MESH,
-        )
-
-    def mark_copy(k):
-        return pltpu.make_async_remote_copy(
-            src_ref=mark, dst_ref=marks.at[b],
-            send_sem=mark_send.at[k], recv_sem=mark_recv.at[k],
-            device_id=(lax.rem(b + k, batches), s), device_id_type=MESH,
-        )
-
-    def start(make, count):
-        def one(k, carry):
-            make(k).start()
-            return carry
-
-        lax.fori_loop(1, count, one, 0)
-
-    def finish(make, count):
-        def one(k, carry):
-            make(k).wait()
-            return carry
-
-        lax.fori_loop(1, count, one, 0)
+    lax.fori_loop(1, devices, greet, 0)
 
     loads[0].wait()
     spread(wide_one, 0, 2, jnp.maximum(maps[0].astype(F32), 0.0))
-    told = jnp.full(mark.shape, index_ref[0].astype(F32))
-    mark[...] = told
-    marks[b] = told
     loads[1].wait()
-    pl.semaphore_wait(barrier, strips + batches - 2)
+    spread(wide_one, 1, 2, jnp.maximum(maps[1].astype(F32), 0.0))
     down = pltpu.make_async_remote_copy(
         src_ref=maps.at[:, rows - 2 : rows], dst_ref=halo.at[0],
         send_sem=halo_send.at[0], recv_sem=halo_recv.at[0],
@@ -139,16 +102,6 @@
         send_sem=halo_send.at[1], recv_sem=halo_recv.at[1],
         device_id=(b, lax.rem(s + strips - 1, strips)), device_id_type=MESH,
     )
-
-    @pl.when(s < strips - 1)
-    def _():
-        down.start()
-
-    @pl.when(s > 0)
-    def _():
-        up.start()
-
-    start(mark_copy, batches)
 
     above = jnp.where(s > 0, 1.0, 0.0)
     below = jnp.where(s < strips - 1, 1.0, 0.0)
@@ -167,12 +120,39 @@
                 piece = jnp.concatenate([piece[: count - 1], piece[count - 1 :] * below], axis=0)
             spread(wide_two, f, r + 1, piece)
 
-    spread(wide_one, 1, 2, jnp.maximum(maps[1].astype(F32), 0.0))
     loads[2].wait()
-    for r, count in chunks(1, rows - 1):
-        first([(0, r, count)])
+    for f in range(2):
+        for r, count in chunks(1, rows - 1):
+            first([(f, r, count)])
+
+    pl.semaphore_wait(barrier, devices - 1)
+
+    @pl.when(s < strips - 1)
+    def _():
+        down.start()
+
+    @pl.when(s > 0)
+    def _():
+        up.start()
+
+    totals = [jnp.zeros((1, channels), F32) for f in range(2)]
+
+    def second(pieces):
+        lhs = [taps(wide_two, f, r, count) for f, r, count in pieces]
+        lhs = lhs[0] if len(lhs) == 1 else jnp.concatenate(lhs, axis=0)
+        out = jnp.dot(lhs, w_two[...], preferred_element_type=F32)
+        at = 0
+        for f, r, count in pieces:
+            skip = maps[f, r : r + count].reshape(count * columns, channels).astype(F32)
+            piece = jnp.maximum(skip + out[at : at + count * columns], 0.0)
+            at += count * columns
+            block_ref[f, 0, r : r + count] = piece.reshape(count, columns, channels)
+            totals[f] = totals[f] + jnp.sum(piece, axis=0, keepdims=True)
 
     loads[3].wait()
+    for f in range(2):
+        for r, count in chunks(2, rows - 2):
+            second([(f, r, count)])
 
     @pl.when(s < strips - 1)
     def _():
@@ -187,37 +167,36 @@
     for f in range(2):
         spread(wide_one, f, 0, jnp.maximum(halo[0, f].astype(F32), 0.0))
         spread(wide_one, f, rows + 2, jnp.maximum(halo[1, f].astype(F32), 0.0))
-    first([(0, -1, 2), (0, rows - 1, 2)])
-    for r, count in chunks(-1, rows + 1):
-        first([(1, r, count)])
-    sums = []
-    for f in range(2):
-        total = jnp.zeros((1, channels), F32)
-        for r, count in chunks(0, rows):
-            skip = maps[f, r : r + count].reshape(count * columns, channels).astype(F32)
-            out = jnp.dot(taps(wide_two, f, r, count), w_two[...], preferred_element_type=F32)
-            out = jnp.maximum(skip + out, 0.0)
-            block_ref[f, 0, r : r + count] = out.reshape(count, columns, channels)
-            total = total + jnp.sum(out, axis=0, keepdims=True)
-        sums.append(total)
-
+    edges = [(f, r) for f in range(2) for r in (0, rows)]
+    first([(f, r - 1, 2) for f, r in edges])
+    second([(f, min(r, rows - 2), 2) for f, r in edges])
+    loads[6].wait()
+    loads[7].wait()
     cells = rows * strips * columns
-    lines = [total[:, LANES * p : LANES * (p + 1)] / cells for total in sums for p in range(packs)]
+    lines = [total[:, LANES * p : LANES * (p + 1)] / cells for total in totals for p in range(packs)]
+    lines.append(jnp.full((1, LANES), index[0].astype(F32)))
+    lines.append(jnp.full((1, LANES), temp[0]))
+    lines.append(jnp.zeros((part.shape[0] - len(lines), LANES), F32))
     share = jnp.concatenate(lines, axis=0)
     part[...] = share
-    parts[s] = share
-    start(part_copy, strips)
-    finish(part_copy, strips)
-    pooled = jnp.sum(parts[...], axis=0).astype(BF)
-    note[...] = pooled
-    notes[b] = pooled
-    start(note_copy, batches)
-    finish(mark_copy, batches)
-    marks_out[...] = jnp.concatenate([marks[i, 0:1] for i in range(batches)], axis=0)
-    finish(note_copy, batches)
-    gathered_ref[...] = notes[...]
+    parts[me] = share
+
+    def send(k, carry):
+        other = lax.rem(me + k, devices)
+        pltpu.make_async_remote_copy(
+            src_ref=part, dst_ref=parts.at[me], send_sem=part_send, recv_sem=part_recv,
+            device_id=(other // strips, lax.rem(other, strips)), device_id_type=MESH,
+        ).start()
+        return carry
+
+    lax.fori_loop(1, devices, send, 0)
     loads[4].wait()
     loads[5].wait()
+    others = parts.at[0 : devices - 1]
+    everyone = pltpu.make_async_copy(others, others, part_recv)
+    everyone.wait()
+    gathered_ref[...] = parts[...]
+    pltpu.make_async_copy(others, others, part_send).wait()
 
 
 def unit_of(emb):
@@ -230,23 +209,27 @@
 
 
 def head_kernel(
-    block_ref, gathered_ref, marks_ref, sproj_ref, gproj_ref, temp_ref,
+    strips, block_ref, gathered_ref, sproj_ref, gproj_ref,
     loss_ref, sgrad_ref, ggrad_ref, out_ref,
     loss, sgrad, ggrad, sem,
 ):
     keep = pltpu.make_async_copy(block_ref, out_ref, sem.at[0])
     keep.start()
-    batches = gathered_ref.shape[0]
+    batches = gathered_ref.shape[0] // strips
     packs = sproj_ref.shape[0] // LANES
-    heard = gathered_ref[...].astype(F32)
+    told = gathered_ref[...].reshape((batches, strips) + gathered_ref.shape[1:])
+    heard = told[:, 0]
+    for i in range(1, strips):
+        heard = heard + told[:, i]
+    heard = heard.astype(BF).astype(F32)
 
     def column(p):
         return jnp.concatenate([heard[i, p : p + 1] for i in range(batches)], axis=0)
 
     state_pool = jnp.concatenate([column(p) for p in range(packs)], axis=1).astype(BF)
     goal_pool = jnp.concatenate([column(packs + p) for p in range(packs)], axis=1).astype(BF)
-    index = marks_ref[:, 0:batches]
-    sharpness = temp_ref[0]
+    index = jnp.concatenate([told[i, 0, 2 * packs : 2 * packs + 1] for i in range(batches)], axis=0)[:, 0:1]
+    sharpness = told[0, 0, 2 * packs + 1 : 2 * packs + 2, 0:1]
     state_unit, state_inverse = unit_of(dot(state_pool, sproj_ref[...], (1, 0)))
     goal_unit, goal_inverse = unit_of(dot(goal_pool, gproj_ref[...], (1, 0)))
     state_bf = state_unit.astype(BF)
@@ -284,11 +267,10 @@
     width = state_proj.shape[1]
     taps_in = conv_one.shape[0] * conv_one.shape[1] * channels
     any_spec = pl.BlockSpec(memory_space=pl.ANY)
-    smem = pl.BlockSpec(memory_space=pltpu.SMEM)
     vmem = pl.BlockSpec(memory_space=pltpu.VMEM)
     block_shape = (2, 1, rows, columns, channels)
     dma = pltpu.SemaphoreType.DMA
-    lines = 2 * channels // LANES
+    lines = 8 * pl.cdiv(2 * channels // LANES + 2, 8)
     stay = [
         pltpu.with_memory_space_constraint(value, pltpu.HBM)
         for value in (
@@ -301,13 +283,12 @@
         functools.partial(block_kernel, batches, strips),
         out_shape=(
             pltpu.VMEM(block_shape, F32),
-            pltpu.VMEM((batches, lines, LANES), BF),
-            pltpu.VMEM((batches, LANES), F32),
+            pltpu.VMEM((batches * strips, lines, LANES), F32),
             pltpu.VMEM((channels, width), BF),
             pltpu.VMEM((channels, width), BF),
         ),
-        in_specs=[any_spec] * 6 + [smem],
-        out_specs=(vmem,) * 5,
+        in_specs=[any_spec] * 8,
+        out_specs=(vmem,) * 4,
         scratch_shapes=[
             pltpu.VMEM((2, rows, columns, channels), BF),
             pltpu.VMEM((2, rows + 4, columns, 3 * channels), BF),
@@ -315,30 +296,27 @@
             pltpu.VMEM((taps_in, channels), BF),
             pltpu.VMEM((taps_in, channels), BF),
             pltpu.VMEM((2, 2, 2, columns, channels), BF),
-            pltpu.VMEM((8, LANES), F32),
-            pltpu.VMEM((batches, 8, LANES), F32),
+            pltpu.SMEM((1,), jnp.int32),
+            pltpu.SMEM((1,), F32),
             pltpu.VMEM((lines, LANES), F32),
-            pltpu.VMEM((strips, lines, LANES), F32),
-            pltpu.VMEM((lines, LANES), BF),
-            pltpu.VMEM((batches, lines, LANES), BF),
-            dma((6,)), dma((2,)), dma((2,)), dma((batches,)), dma((batches,)),
-            dma((strips,)), dma((strips,)), dma((batches,)), dma((batches,)),
+            pltpu.VMEM((batches * strips, lines, LANES), F32),
+            dma((8,)), dma((2,)), dma((2,)), dma(()), dma(()),
         ],
         compiler_params=pltpu.CompilerParams(
             collective_id=0, has_side_effects=True, vmem_limit_bytes=40 * 2**20
         ),
         name="block",
-    )(*stay, pair_index)
+    )(*stay, pair_index, inv_temp)
     held = [pltpu.with_memory_space_constraint(value, pltpu.VMEM) for value in held]
     return pl.pallas_call(
-        head_kernel,
+        functools.partial(head_kernel, strips),
         out_shape=(
             jax.ShapeDtypeStruct((1,), F32),
             jax.ShapeDtypeStruct((channels, width), F32),
             jax.ShapeDtypeStruct((channels, width), F32),
             jax.ShapeDtypeStruct(block_shape, F32),
         ),
-        in_specs=[vmem] * 5 + [smem],
+        in_specs=[vmem] * 4,
         out_specs=(any_spec,) * 4,
         scratch_shapes=[
             pltpu.SMEM((1,), F32),
@@ -348,7 +326,7 @@
         ],
         compiler_params=pltpu.CompilerParams(vmem_limit_bytes=40 * 2**20),
         name="head",
-    )(*held, inv_temp)
+    )(*held)
 
 
 def solution(mesh):

time: 22.5 us -> 21.9 us (0.973)
  Pallas kernels: 20.4 us -> 19.8 us
    pallas_call x1, Pallas kernels: 18.1 us -> 17.4 us  [shards(): pl.pallas_call(functools.partial(block_kernel, batches, strips), out_shap...]
where the time goes in v1:
time: 21.9 us; the launch traced here: 21.7 us
  Pallas kernels  19.8 us (90%)
  between operations  1.93 us (9%)
    pallas_call x1, Pallas kernels, shards(): pl.pallas_call(functools.partial(block_kernel, batches, strips), out_shap...  17.4 us
    pallas_call x1, Pallas kernels, shards(): pl.pallas_call(functools.partial(head_kernel, strips), out_shape=(jax.Sha...  2.38 us

profile of v1, /device:TPU:0, one launch (start us, length us, event | category | flops | bytes accessed | tf_op | source)
XLA Modules:
  0.0 21.7 jit_solution(9925459044879344032)
XLA Ops:
  1.9 17.4 %block.1 = (f32[2,1,16,64,256]{4,3,2,1,0:T(8,128)S(1)}, f32[32,8,128]{2,1,0:T(8,128)S(1)}, bf16[256,1024]{1,0:T(8,128)(2,1)S(1)}, bf16[256,1024]{1,0:T(8,128)(2,1)S(1)}) custom-call(bf16[1,16,64,256]{3,2,1,0:T(8,128)(2,1)} %state_ref.1, bf16[1,16,64,256]{3,2,1,0:T(8,128)(2,1)} %goal_ref.1, bf16[2304,256]{1,0:T(8,128)(2,1)} %bitcast.2, ...), custom_call_target="tpu_custom_call" | custom-call | tf_op jit(solution)/shard_map/block/pallas_call | solution.py:282
  19.3 2.4 %head.1 = (f32[1]{0:T(128)}, f32[256,1024]{1,0:T(8,128)}, f32[256,1024]{1,0:T(8,128)}, f32[2,1,16,64,256]{4,3,2,1,0:T(8,128)}) custom-call(f32[2,1,16,64,256]{4,3,2,1,0:T(8,128)S(1)} %get-tuple-element.8.block_ref, f32[32,8,128]{2,1,0:T(8,128)S(1)} %get-tuple-element.9.gathered_ref, bf16[256,1024]{1,0:T(8,128)(2,1)S(1)} %get-tuple-element.10.sproj_ref, ...), custom_call_target="tpu_custom_call" | custom-call | tf_op jit(solution)/shard_map/head/pallas_call | solution.py:311

commit v2 on v1

--- a/solution.py
+++ b/solution.py
@@ -11,39 +11,82 @@
 BF = jnp.bfloat16
 F32 = jnp.float32
 LANES = 128
-ROWS_AT_ONCE = 6
-
-
-def spread(dst, frame, row, cells):
-    rows, columns, channels = cells.shape
-    where = lax.broadcasted_iota(jnp.int32, cells.shape, 1)
-    left = jnp.where(where == 0, 0.0, pltpu.roll(cells, 1, axis=1))
-    right = jnp.where(where == columns - 1, 0.0, pltpu.roll(cells, columns - 1, axis=1))
-    span = pl.ds(row, rows)
-    dst[frame, span, :, 0:channels] = left.astype(BF)
-    dst[frame, span, :, channels : 2 * channels] = cells.astype(BF)
-    dst[frame, span, :, 2 * channels : 3 * channels] = right.astype(BF)
-
-
-def chunks(start, stop):
-    number = -(-(stop - start) // ROWS_AT_ONCE)
-    cuts = [start + (stop - start) * i // number for i in range(number + 1)]
-    return [(low, high - low) for low, high in zip(cuts, cuts[1:])]
-
-
-def taps(src, frame, row, rows):
-    columns, width = src.shape[2], src.shape[3]
+PAD = 8
+
+
+def taps(store, k, frame, row, rows):
+    pairs, channels = store.shape[3], store.shape[4]
     return jnp.concatenate(
-        [src[frame, row + d : row + d + rows].reshape(rows * columns, width) for d in range(3)],
+        [store[k, frame, row + d : row + d + rows].reshape(rows * pairs, channels) for d in range(3)],
         axis=1,
     )
+
+
+def stage(raw, frame, row, cells):
+    columns = cells.shape[1]
+    cells = cells.astype(F32)
+    for h in range(raw.shape[2]):
+        raw[frame, row : row + cells.shape[0], h, PAD : PAD + columns] = cells[:, :, LANES * h : LANES * (h + 1)]
+
+
+def halved(raw, frame, row, first):
+    pairs = (raw.shape[3] - 2 * PAD) // 2
+    return [raw[frame, row, h, pl.ds(PAD + first, pairs, stride=2)] for h in range(raw.shape[2])]
+
+
+def widen(store, raw, frame, rows):
+    for row in rows:
+        parts = [[jnp.maximum(x, 0.0) for x in halved(raw, frame, row, first)] for first in (-1, 0, 1, 2)]
+        for h, (before, even, odd, after) in enumerate(zip(*parts)):
+            lanes = slice(LANES * h, LANES * (h + 1))
+            for k, value in enumerate((before - odd, even + odd, odd - even, even - after)):
+                store[k, frame, row, :, lanes] = value.astype(BF)
+
+
+def spread(store, frame, row, even, odd):
+    rows, pairs, _ = even.shape
+    where = lax.broadcasted_iota(jnp.int32, even.shape, 1)
+    before = jnp.where(where == 0, 0.0, pltpu.roll(odd, 1, axis=1))
+    after = jnp.where(where == pairs - 1, 0.0, pltpu.roll(even, pairs - 1, axis=1))
+    span = slice(row, row + rows)
+    for k, value in enumerate((before - odd, even + odd, odd - even, even - after)):
+        store[k, frame, span] = value.astype(BF)
+
+
+def mix(mixed, w):
+    channels = w.shape[1]
+    for d in range(3):
+        left, centre, right = (
+            w[(3 * d + c) * channels : (3 * d + c + 1) * channels].astype(F32) for c in range(3)
+        )
+        outer, inner = 0.5 * (left + right), 0.5 * centre
+        span = slice(d * channels, (d + 1) * channels)
+        mixed[0, span] = (outer + inner).astype(BF)
+        mixed[1, span] = (outer - inner).astype(BF)
+
+
+def products(store, w, mixed, pieces):
+    channels = w.shape[1]
+    out = []
+    for k in range(4):
+        lhs = [taps(store, k, f, r, count) for f, r, count in pieces]
+        lhs = lhs[0] if len(lhs) == 1 else jnp.concatenate(lhs, axis=0)
+        if k in (0, 3):
+            c = 0 if k == 0 else 2
+            rhs = jnp.concatenate(
+                [w[(3 * d + c) * channels : (3 * d + c + 1) * channels] for d in range(3)], axis=0
+            )
+        else:
+            rhs = mixed[k - 1]
+        out.append(jnp.dot(lhs, rhs, preferred_element_type=F32))
+    return (out[1] + out[2]) + out[0], (out[1] - out[2]) - out[3]
 
 
 def block_kernel(
     batches, strips,
     state_ref, goal_ref, one_ref, two_ref, sproj_ref, gproj_ref, index_ref, temp_ref,
     block_ref, gathered_ref, sproj_out, gproj_out,
-    maps, wide_one, wide_two, w_one, w_two, halo, index, temp, part, parts,
+    maps, raw, wide_one, wide_two, w_one, w_two, mixed_one, mixed_two, halo, index, temp, part, parts,
     load_sem, halo_send, halo_recv, part_send, part_recv,
 ):
     b = lax.axis_index("batch")
@@ -57,8 +100,8 @@
         pltpu.make_async_copy(source, target, load_sem.at[i])
         for i, (source, target) in enumerate((
             (state_ref.at[0], maps.at[0]),
+            (one_ref, w_one),
             (goal_ref.at[0], maps.at[1]),
-            (one_ref, w_one),
             (two_ref, w_two),
             (sproj_ref, sproj_out),
             (gproj_ref, gproj_out),
@@ -87,11 +130,18 @@
         return carry
 
     lax.fori_loop(1, devices, greet, 0)
+    edge = jnp.zeros((raw.shape[1], raw.shape[2], PAD, LANES), F32)
+    for f in range(2):
+        raw[f, :, :, 0:PAD] = edge
+        raw[f, :, :, PAD + columns :] = edge
 
     loads[0].wait()
-    spread(wide_one, 0, 2, jnp.maximum(maps[0].astype(F32), 0.0))
+    stage(raw, 0, 2, maps[0])
+    widen(wide_one, raw, 0, range(2, rows + 2))
     loads[1].wait()
-    spread(wide_one, 1, 2, jnp.maximum(maps[1].astype(F32), 0.0))
+    mix(mixed_one, w_one)
+    loads[2].wait()
+    stage(raw, 1, 2, maps[1])
     down = pltpu.make_async_remote_copy(
         src_ref=maps.at[:, rows - 2 : rows], dst_ref=halo.at[0],
         send_sem=halo_send.at[0], recv_sem=halo_recv.at[0],
@@ -106,53 +156,58 @@
     above = jnp.where(s > 0, 1.0, 0.0)
     below = jnp.where(s < strips - 1, 1.0, 0.0)
 
+    pairs = columns // 2
+
     def first(pieces):
-        lhs = [taps(wide_one, f, r + 1, count) for f, r, count in pieces]
-        lhs = lhs[0] if len(lhs) == 1 else jnp.concatenate(lhs, axis=0)
-        out = jnp.maximum(jnp.dot(lhs, w_one[...], preferred_element_type=F32), 0.0)
+        evens, odds = products(wide_one, w_one, mixed_one, [(f, r + 1, count) for f, r, count in pieces])
         at = 0
         for f, r, count in pieces:
-            piece = out[at : at + count * columns].reshape(count, columns, channels)
-            at += count * columns
-            if r < 0:
-                piece = jnp.concatenate([piece[0:1] * above, piece[1:]], axis=0)
-            if r + count > rows:
-                piece = jnp.concatenate([piece[: count - 1], piece[count - 1 :] * below], axis=0)
-            spread(wide_two, f, r + 1, piece)
-
-    loads[2].wait()
-    for f in range(2):
-        for r, count in chunks(1, rows - 1):
-            first([(f, r, count)])
-
-    pl.semaphore_wait(barrier, devices - 1)
-
-    @pl.when(s < strips - 1)
-    def _():
-        down.start()
-
-    @pl.when(s > 0)
-    def _():
-        up.start()
-
-    totals = [jnp.zeros((1, channels), F32) for f in range(2)]
+            both = []
+            for out in (evens, odds):
+                piece = jnp.maximum(out[at : at + count * pairs], 0.0).reshape(count, pairs, channels)
+                if r < 0:
+                    piece = jnp.concatenate([piece[0:1] * above, piece[1:]], axis=0)
+                if r + count > rows:
+                    piece = jnp.concatenate([piece[: count - 1], piece[count - 1 :] * below], axis=0)
+                both.append(piece)
+            at += count * pairs
+            spread(wide_two, f, r + 1, *both)
+
+    first([(0, 1, rows - 2)])
+    widen(wide_one, raw, 1, range(2, rows + 2))
+    first([(1, 1, rows - 2)])
+    loads[3].wait()
+    mix(mixed_two, w_two)
 
     def second(pieces):
-        lhs = [taps(wide_two, f, r, count) for f, r, count in pieces]
-        lhs = lhs[0] if len(lhs) == 1 else jnp.concatenate(lhs, axis=0)
-        out = jnp.dot(lhs, w_two[...], preferred_element_type=F32)
+        evens, odds = products(wide_two, w_two, mixed_two, pieces)
         at = 0
         for f, r, count in pieces:
-            skip = maps[f, r : r + count].reshape(count * columns, channels).astype(F32)
-            piece = jnp.maximum(skip + out[at : at + count * columns], 0.0)
-            at += count * columns
-            block_ref[f, 0, r : r + count] = piece.reshape(count, columns, channels)
-            totals[f] = totals[f] + jnp.sum(piece, axis=0, keepdims=True)
-
-    loads[3].wait()
-    for f in range(2):
-        for r, count in chunks(2, rows - 2):
-            second([(f, r, count)])
+            for first, out in enumerate((evens, odds)):
+                piece = out[at : at + count * pairs]
+                for i in range(count):
+                    skips = halved(raw, f, r + 2 + i, first)
+                    for h, skip in enumerate(skips):
+                        lanes = slice(LANES * h, LANES * (h + 1))
+                        value = jnp.maximum(skip + piece[i * pairs : (i + 1) * pairs, lanes], 0.0)
+                        block_ref[f, r + i, h, pl.ds(first, pairs, stride=2)] = value
+                        totals[f][h] = totals[f][h] + value
+            at += count * pairs
+
+    totals = [[jnp.zeros((pairs, LANES), F32) for h in range(packs)] for f in range(2)]
+    second([(0, 2, rows - 4)])
+
+    pl.semaphore_wait(barrier, devices - 1)
+
+    @pl.when(s < strips - 1)
+    def _():
+        down.start()
+
+    @pl.when(s > 0)
+    def _():
+        up.start()
+
+    second([(1, 2, rows - 4)])
 
     @pl.when(s < strips - 1)
     def _():
@@ -165,15 +220,16 @@
         down.wait_recv()
 
     for f in range(2):
-        spread(wide_one, f, 0, jnp.maximum(halo[0, f].astype(F32), 0.0))
-        spread(wide_one, f, rows + 2, jnp.maximum(halo[1, f].astype(F32), 0.0))
+        stage(raw, f, 0, halo[0, f])
+        stage(raw, f, rows + 2, halo[1, f])
+        widen(wide_one, raw, f, (0, 1, rows + 2, rows + 3))
     edges = [(f, r) for f in range(2) for r in (0, rows)]
     first([(f, r - 1, 2) for f, r in edges])
     second([(f, min(r, rows - 2), 2) for f, r in edges])
     loads[6].wait()
     loads[7].wait()
     cells = rows * strips * columns
-    lines = [total[:, LANES * p : LANES * (p + 1)] / cells for total in totals for p in range(packs)]
+    lines = [jnp.sum(total, axis=0, keepdims=True) / cells for frame in totals for total in frame]
     lines.append(jnp.full((1, LANES), index[0].astype(F32)))
     lines.append(jnp.full((1, LANES), temp[0]))
     lines.append(jnp.zeros((part.shape[0] - len(lines), LANES), F32))
@@ -181,15 +237,22 @@
     part[...] = share
     parts[me] = share
 
+    facing = devices - 1 - me
+    way = devices - 1 - (devices - 2) * (2 * me // devices)
+
     def send(k, carry):
-        other = lax.rem(me + k, devices)
-        pltpu.make_async_remote_copy(
-            src_ref=part, dst_ref=parts.at[me], send_sem=part_send, recv_sem=part_recv,
-            device_id=(other // strips, lax.rem(other, strips)), device_id_type=MESH,
-        ).start()
+        other = lax.rem(facing + k * way, devices)
+
+        @pl.when(other != me)
+        def _():
+            pltpu.make_async_remote_copy(
+                src_ref=part, dst_ref=parts.at[me], send_sem=part_send, recv_sem=part_recv,
+                device_id=(other // strips, lax.rem(other, strips)), device_id_type=MESH,
+            ).start()
+
         return carry
 
-    lax.fori_loop(1, devices, send, 0)
+    lax.fori_loop(0, devices, send, 0)
     loads[4].wait()
     loads[5].wait()
     others = parts.at[0 : devices - 1]
@@ -213,8 +276,14 @@
     loss_ref, sgrad_ref, ggrad_ref, out_ref,
     loss, sgrad, ggrad, sem,
 ):
-    keep = pltpu.make_async_copy(block_ref, out_ref, sem.at[0])
-    keep.start()
+    copies = [
+        pltpu.make_async_copy(
+            block_ref.at[:, :, h], out_ref.at[:, 0, :, :, LANES * h : LANES * (h + 1)], sem.at[h]
+        )
+        for h in range(block_ref.shape[2])
+    ]
+    for copy in copies:
+        copy.start()
     batches = gathered_ref.shape[0] // strips
     packs = sproj_ref.shape[0] // LANES
     told = gathered_ref[...].reshape((batches, strips) + gathered_ref.shape[1:])
@@ -242,10 +311,9 @@
     losses = jnp.log(row_total) - positive
     mine = lax.broadcasted_iota(jnp.int32, losses.shape, 0) == lax.axis_index("batch")
     loss[0] = jnp.sum(jnp.where(mine, losses, 0.0))
-    say = pltpu.make_async_copy(loss, loss_ref, sem.at[1])
-    say.start()
+    copies.append(pltpu.make_async_copy(loss, loss_ref, sem.at[len(copies)]))
+    copies[-1].start()
     logit_grad = (exp_logits / row_total - matched.astype(F32)).astype(BF)
-    copies = [keep, say]
     for pool, unit, inverse, unit_grad, grad, target in (
         (state_pool, state_unit, state_inverse, dot(logit_grad, goal_bf, (1, 0)), sgrad, sgrad_ref),
         (goal_pool, goal_unit, goal_inverse, dot(logit_grad, state_bf, (0, 0)), ggrad, ggrad_ref),
@@ -268,7 +336,7 @@
     taps_in = conv_one.shape[0] * conv_one.shape[1] * channels
     any_spec = pl.BlockSpec(memory_space=pl.ANY)
     vmem = pl.BlockSpec(memory_space=pltpu.VMEM)
-    block_shape = (2, 1, rows, columns, channels)
+    packs = channels // LANES
     dma = pltpu.SemaphoreType.DMA
     lines = 8 * pl.cdiv(2 * channels // LANES + 2, 8)
     stay = [
@@ -282,7 +350,7 @@
     held = pl.pallas_call(
         functools.partial(block_kernel, batches, strips),
         out_shape=(
-            pltpu.VMEM(block_shape, F32),
+            pltpu.VMEM((2, rows, packs, columns, LANES), F32),
             pltpu.VMEM((batches * strips, lines, LANES), F32),
             pltpu.VMEM((channels, width), BF),
             pltpu.VMEM((channels, width), BF),
@@ -291,10 +359,13 @@
         out_specs=(vmem,) * 4,
         scratch_shapes=[
             pltpu.VMEM((2, rows, columns, channels), BF),
-            pltpu.VMEM((2, rows + 4, columns, 3 * channels), BF),
-            pltpu.VMEM((2, rows + 2, columns, 3 * channels), BF),
+            pltpu.VMEM((2, rows + 4, packs, columns + 2 * PAD, LANES), F32),
+            pltpu.VMEM((4, 2, rows + 4, columns // 2, channels), BF),
+            pltpu.VMEM((4, 2, rows + 2, columns // 2, channels), BF),
             pltpu.VMEM((taps_in, channels), BF),
             pltpu.VMEM((taps_in, channels), BF),
+            pltpu.VMEM((2, taps_in // 3, channels), BF),
+            pltpu.VMEM((2, taps_in // 3, channels), BF),
             pltpu.VMEM((2, 2, 2, columns, channels), BF),
             pltpu.SMEM((1,), jnp.int32),
             pltpu.SMEM((1,), F32),
@@ -314,7 +385,7 @@
             jax.ShapeDtypeStruct((1,), F32),
             jax.ShapeDtypeStruct((channels, width), F32),
             jax.ShapeDtypeStruct((channels, width), F32),
-            jax.ShapeDtypeStruct(block_shape, F32),
+            jax.ShapeDtypeStruct((2, 1, rows, columns, channels), F32),
         ),
         in_specs=[vmem] * 4,
         out_specs=(any_spec,) * 4,
@@ -322,7 +393,7 @@
             pltpu.SMEM((1,), F32),
             pltpu.VMEM((channels, width), F32),
             pltpu.VMEM((channels, width), F32),
-            dma((2 + 2 * (channels // LANES),)),
+            dma((1 + 3 * (channels // LANES),)),
         ],
         compiler_params=pltpu.CompilerParams(vmem_limit_bytes=40 * 2**20),
         name="head",

time: 21.9 us -> 21.9 us (level)
  no operation moved by 1% of the time
where the time goes in v2:
time: 21.9 us; the launch traced here: 21.8 us
  Pallas kernels  19.8 us (90%)
  between operations  1.93 us (9%)
    pallas_call x1, Pallas kernels, shards(): pl.pallas_call(functools.partial(block_kernel, batches, strips), out_shap...  17.4 us
    pallas_call x1, Pallas kernels, shards(): pl.pallas_call(functools.partial(head_kernel, strips), out_shape=(jax.Sha...  2.4 us

profile of v2, /device:TPU:0, one launch (start us, length us, event | category | flops | bytes accessed | tf_op | source)
XLA Modules:
  0.0 21.8 jit_solution(14065334342000621152)
XLA Ops:
  1.9 17.4 %block.1 = (f32[2,16,2,64,128]{4,3,2,1,0:T(8,128)S(1)}, f32[32,8,128]{2,1,0:T(8,128)S(1)}, bf16[256,1024]{1,0:T(8,128)(2,1)S(1)}, bf16[256,1024]{1,0:T(8,128)(2,1)S(1)}) custom-call(bf16[1,16,64,256]{3,2,1,0:T(8,128)(2,1)} %state_ref.1, bf16[1,16,64,256]{3,2,1,0:T(8,128)(2,1)} %goal_ref.1, bf16[2304,256]{1,0:T(8,128)(2,1)} %bitcast.2, ...), custom_call_target="tpu_custom_call" | custom-call | tf_op jit(solution)/shard_map/block/pallas_call | solution.py:350
  19.4 2.4 %head.1 = (f32[1]{0:T(128)}, f32[256,1024]{1,0:T(8,128)}, f32[256,1024]{1,0:T(8,128)}, f32[2,1,16,64,256]{4,3,2,1,0:T(8,128)}) custom-call(f32[2,16,2,64,128]{4,3,2,1,0:T(8,128)S(1)} %get-tuple-element.8.block_ref, f32[32,8,128]{2,1,0:T(8,128)S(1)} %get-tuple-element.9.gathered_ref, bf16[256,1024]{1,0:T(8,128)(2,1)S(1)} %get-tuple-element.10.sproj_ref, ...), custom_call_target="tpu_custom_call" | custom-call | tf_op jit(solution)/shard_map/head/pallas_call | solution.py:382

commit v3 on v2

--- a/solution.py
+++ b/solution.py
@@ -85,9 +85,9 @@
 def block_kernel(
     batches, strips,
     state_ref, goal_ref, one_ref, two_ref, sproj_ref, gproj_ref, index_ref, temp_ref,
-    block_ref, gathered_ref, sproj_out, gproj_out,
-    maps, raw, wide_one, wide_two, w_one, w_two, mixed_one, mixed_two, halo, index, temp, part, parts,
-    load_sem, halo_send, halo_recv, part_send, part_recv,
+    block_ref, gathered_ref, marks_out, sproj_out, gproj_out,
+    maps, raw, wide_one, wide_two, w_one, w_two, mixed_one, mixed_two, halo, index, temp, mark, marks, part, parts,
+    load_sem, halo_send, halo_recv, mark_send, mark_recv, part_send, part_recv,
 ):
     b = lax.axis_index("batch")
     s = lax.axis_index("strip")
@@ -173,12 +173,6 @@
             at += count * pairs
             spread(wide_two, f, r + 1, *both)
 
-    first([(0, 1, rows - 2)])
-    widen(wide_one, raw, 1, range(2, rows + 2))
-    first([(1, 1, rows - 2)])
-    loads[3].wait()
-    mix(mixed_two, w_two)
-
     def second(pieces):
         evens, odds = products(wide_two, w_two, mixed_two, pieces)
         at = 0
@@ -195,18 +189,51 @@
             at += count * pairs
 
     totals = [[jnp.zeros((pairs, LANES), F32) for h in range(packs)] for f in range(2)]
+    first([(0, 1, rows - 2)])
+    widen(wide_one, raw, 1, range(2, rows + 2))
+    first([(1, 1, rows - 2)])
+
+    pl.semaphore_wait(barrier, devices - 1)
+    loads[6].wait()
+    told = jnp.full(mark.shape, index[0].astype(F32))
+    mark[...] = told
+    marks[b] = told
+    own = 2 * b // batches
+    way = batches - 1 - (batches - 2) * own
+    first_peer = (batches - 1) * (1 - own)
+
+    def peers(make):
+        def one(k, carry):
+            other = lax.rem(first_peer + k * way, batches)
+
+            @pl.when(other != b)
+            def _():
+                make(other).start()
+
+            return carry
+
+        lax.fori_loop(0, batches, one, 0)
+
+    def settle(buffer, sem, count):
+        if count:
+            pltpu.make_async_copy(buffer.at[0:count], buffer.at[0:count], sem).wait()
+
+    peers(lambda other: pltpu.make_async_remote_copy(
+        src_ref=mark, dst_ref=marks.at[b], send_sem=mark_send, recv_sem=mark_recv,
+        device_id=(other, s), device_id_type=MESH,
+    ))
+
+    @pl.when(s < strips - 1)
+    def _():
+        down.start()
+
+    @pl.when(s > 0)
+    def _():
+        up.start()
+
+    loads[3].wait()
+    mix(mixed_two, w_two)
     second([(0, 2, rows - 4)])
-
-    pl.semaphore_wait(barrier, devices - 1)
-
-    @pl.when(s < strips - 1)
-    def _():
-        down.start()
-
-    @pl.when(s > 0)
-    def _():
-        up.start()
-
     second([(1, 2, rows - 4)])
 
     @pl.when(s < strips - 1)
@@ -226,22 +253,17 @@
     edges = [(f, r) for f in range(2) for r in (0, rows)]
     first([(f, r - 1, 2) for f, r in edges])
     second([(f, min(r, rows - 2), 2) for f, r in edges])
-    loads[6].wait()
-    loads[7].wait()
     cells = rows * strips * columns
     lines = [jnp.sum(total, axis=0, keepdims=True) / cells for frame in totals for total in frame]
-    lines.append(jnp.full((1, LANES), index[0].astype(F32)))
-    lines.append(jnp.full((1, LANES), temp[0]))
-    lines.append(jnp.zeros((part.shape[0] - len(lines), LANES), F32))
     share = jnp.concatenate(lines, axis=0)
     part[...] = share
     parts[me] = share
-
-    facing = devices - 1 - me
-    way = devices - 1 - (devices - 2) * (2 * me // devices)
+    high = 2 * me // devices
+    stride = devices - 1 - (devices - 2) * high
+    nearest = (devices - 1) * (1 - high)
 
     def send(k, carry):
-        other = lax.rem(facing + k * way, devices)
+        other = lax.rem(nearest + k * stride, devices)
 
         @pl.when(other != me)
         def _():
@@ -253,13 +275,15 @@
         return carry
 
     lax.fori_loop(0, devices, send, 0)
-    loads[4].wait()
-    loads[5].wait()
-    others = parts.at[0 : devices - 1]
-    everyone = pltpu.make_async_copy(others, others, part_recv)
-    everyone.wait()
+    for i in (4, 5, 7):
+        loads[i].wait()
+    settle(marks, mark_recv, batches - 1)
+    settle(marks, mark_send, batches - 1)
+    marks_out[0:batches] = marks[...]
+    marks_out[batches] = jnp.full(mark.shape, temp[0])
+    settle(parts, part_recv, devices - 1)
     gathered_ref[...] = parts[...]
-    pltpu.make_async_copy(others, others, part_send).wait()
+    settle(parts, part_send, devices - 1)
 
 
 def unit_of(emb):
@@ -272,7 +296,7 @@
 
 
 def head_kernel(
-    strips, block_ref, gathered_ref, sproj_ref, gproj_ref,
+    strips, block_ref, gathered_ref, marks_ref, sproj_ref, gproj_ref,
     loss_ref, sgrad_ref, ggrad_ref, out_ref,
     loss, sgrad, ggrad, sem,
 ):
@@ -297,8 +321,8 @@
 
     state_pool = jnp.concatenate([column(p) for p in range(packs)], axis=1).astype(BF)
     goal_pool = jnp.concatenate([column(packs + p) for p in range(packs)], axis=1).astype(BF)
-    index = jnp.concatenate([told[i, 0, 2 * packs : 2 * packs + 1] for i in range(batches)], axis=0)[:, 0:1]
-    sharpness = told[0, 0, 2 * packs + 1 : 2 * packs + 2, 0:1]
+    index = jnp.concatenate([marks_ref[i] for i in range(batches)], axis=0)[:, 0:1]
+    sharpness = marks_ref[batches][:, 0:1]
     state_unit, state_inverse = unit_of(dot(state_pool, sproj_ref[...], (1, 0)))
     goal_unit, goal_inverse = unit_of(dot(goal_pool, gproj_ref[...], (1, 0)))
     state_bf = state_unit.astype(BF)
@@ -338,7 +362,7 @@
     vmem = pl.BlockSpec(memory_space=pltpu.VMEM)
     packs = channels // LANES
     dma = pltpu.SemaphoreType.DMA
-    lines = 8 * pl.cdiv(2 * channels // LANES + 2, 8)
+    lines = 2 * packs
     stay = [
         pltpu.with_memory_space_constraint(value, pltpu.HBM)
         for value in (
@@ -352,11 +376,12 @@
         out_shape=(
             pltpu.VMEM((2, rows, packs, columns, LANES), F32),
             pltpu.VMEM((batches * strips, lines, LANES), F32),
+            pltpu.VMEM((batches + 1, 1, LANES), F32),
             pltpu.VMEM((channels, width), BF),
             pltpu.VMEM((channels, width), BF),
         ),
         in_specs=[any_spec] * 8,
-        out_specs=(vmem,) * 4,
+        out_specs=(vmem,) * 5,
         scratch_shapes=[
             pltpu.VMEM((2, rows, columns, channels), BF),
             pltpu.VMEM((2, rows + 4, packs, columns + 2 * PAD, LANES), F32),
@@ -369,9 +394,11 @@
             pltpu.VMEM((2, 2, 2, columns, channels), BF),
             pltpu.SMEM((1,), jnp.int32),
             pltpu.SMEM((1,), F32),
+            pltpu.VMEM((1, LANES), F32),
+            pltpu.VMEM((batches, 1, LANES), F32),
             pltpu.VMEM((lines, LANES), F32),
             pltpu.VMEM((batches * strips, lines, LANES), F32),
-            dma((8,)), dma((2,)), dma((2,)), dma(()), dma(()),
+            dma((8,)), dma((2,)), dma((2,)), dma(()), dma(()), dma(()), dma(()),
         ],
         compiler_params=pltpu.CompilerParams(
             collective_id=0, has_side_effects=True, vmem_limit_bytes=40 * 2**20
@@ -387,7 +414,7 @@
             jax.ShapeDtypeStruct((channels, width), F32),
             jax.ShapeDtypeStruct((2, 1, rows, columns, channels), F32),
         ),
-        in_specs=[vmem] * 4,
+        in_specs=[vmem] * 5,
         out_specs=(any_spec,) * 4,
         scratch_shapes=[
             pltpu.SMEM((1,), F32),

time: 21.9 us -> 20 us (0.913)
  Pallas kernels: 19.8 us -> 17.9 us
    pallas_call x1, Pallas kernels: 17.4 us -> 15.6 us  [shards(): pl.pallas_call(functools.partial(block_kernel, batches, strips), out_shap...]
where the time goes in v3:
time: 20 us; the launch traced here: 19.9 us
  Pallas kernels  17.9 us (89%)
  between operations  1.93 us (10%)
    pallas_call x1, Pallas kernels, shards(): pl.pallas_call(functools.partial(block_kernel, batches, strips), out_shap...  15.6 us
    pallas_call x1, Pallas kernels, shards(): pl.pallas_call(functools.partial(head_kernel, strips), out_shape=(jax.Sha...  2.4 us

profile of v3, /device:TPU:0, one launch (start us, length us, event | category | flops | bytes accessed | tf_op | source)
XLA Modules:
  0.0 19.9 jit_solution(5110871802840948906)
XLA Ops:
  1.9 15.6 %block.1 = (f32[2,16,2,64,128]{4,3,2,1,0:T(8,128)S(1)}, f32[32,4,128]{2,1,0:T(4,128)S(1)}, f32[17,1,128]{2,1,0:T(1,128)S(1)}, bf16[256,1024]{1,0:T(8,128)(2,1)S(1)}, bf16[256,1024]{1,0:T(8,128)(2,1)S(1)}) custom-call(bf16[1,16,64,256]{3,2,1,0:T(8,128)(2,1)} %state_ref.1, bf16[1,16,64,256]{3,2,1,0:T(8,128)(2,1)} %goal_ref.1, bf16[2304,256]{1,0:T(8,128)(2,1)} %bitcast.2, ...), custom_call_target="tpu_custom_call" | custom-call | tf_op jit(solution)/shard_map/block/pallas_call | solution.py:374
  17.5 2.4 %head.1 = (f32[1]{0:T(128)}, f32[256,1024]{1,0:T(8,128)}, f32[256,1024]{1,0:T(8,128)}, f32[2,1,16,64,256]{4,3,2,1,0:T(8,128)}) custom-call(f32[2,16,2,64,128]{4,3,2,1,0:T(8,128)S(1)} %get-tuple-element.9.block_ref, f32[32,4,128]{2,1,0:T(4,128)S(1)} %get-tuple-element.10.gathered_ref, f32[17,1,128]{2,1,0:T(1,128)S(1)} %get-tuple-element.11.marks_ref, ...), custom_call_target="tpu_custom_call" | custom-call | tf_op jit(solution)/shard_map/head/pallas_call | solution.py:409

commit v4 on v3

--- a/solution.py
+++ b/solution.py
@@ -67,8 +67,8 @@
 
 def products(store, w, mixed, pieces):
     channels = w.shape[1]
-    out = []
-    for k in range(4):
+    out = [None] * 4
+    for k in (0, 3, 1, 2):
         lhs = [taps(store, k, f, r, count) for f, r, count in pieces]
         lhs = lhs[0] if len(lhs) == 1 else jnp.concatenate(lhs, axis=0)
         if k in (0, 3):
@@ -78,7 +78,11 @@
             )
         else:
             rhs = mixed[k - 1]
-        out.append(jnp.dot(lhs, rhs, preferred_element_type=F32))
+        out[k] = jnp.dot(lhs, rhs, preferred_element_type=F32)
+    return out
+
+
+def combine(out):
     return (out[1] + out[2]) + out[0], (out[1] - out[2]) - out[3]
 
 
@@ -100,8 +104,8 @@
         pltpu.make_async_copy(source, target, load_sem.at[i])
         for i, (source, target) in enumerate((
             (state_ref.at[0], maps.at[0]),
+            (goal_ref.at[0], maps.at[1]),
             (one_ref, w_one),
-            (goal_ref.at[0], maps.at[1]),
             (two_ref, w_two),
             (sproj_ref, sproj_out),
             (gproj_ref, gproj_out),
@@ -123,25 +127,19 @@
     barrier = pltpu.get_barrier_semaphore()
 
     def greet(k, carry):
-        other = lax.rem(me + k, devices)
-        pl.semaphore_signal(
-            barrier, inc=1, device_id=(other // strips, lax.rem(other, strips)), device_id_type=MESH
-        )
+        other = lax.rem(b + k, batches)
+        for t in range(strips):
+            pl.semaphore_signal(barrier, inc=1, device_id=(other, t), device_id_type=MESH)
         return carry
 
-    lax.fori_loop(1, devices, greet, 0)
+    for t in range(1, strips):
+        pl.semaphore_signal(barrier, inc=1, device_id=(b, lax.rem(s + t, strips)), device_id_type=MESH)
+    lax.fori_loop(1, batches, greet, 0)
     edge = jnp.zeros((raw.shape[1], raw.shape[2], PAD, LANES), F32)
     for f in range(2):
         raw[f, :, :, 0:PAD] = edge
         raw[f, :, :, PAD + columns :] = edge
 
-    loads[0].wait()
-    stage(raw, 0, 2, maps[0])
-    widen(wide_one, raw, 0, range(2, rows + 2))
-    loads[1].wait()
-    mix(mixed_one, w_one)
-    loads[2].wait()
-    stage(raw, 1, 2, maps[1])
     down = pltpu.make_async_remote_copy(
         src_ref=maps.at[:, rows - 2 : rows], dst_ref=halo.at[0],
         send_sem=halo_send.at[0], recv_sem=halo_recv.at[0],
@@ -155,11 +153,16 @@
 
     above = jnp.where(s > 0, 1.0, 0.0)
     below = jnp.where(s < strips - 1, 1.0, 0.0)
-
     pairs = columns // 2
+    inner = range(2, rows + 2)
+    outer = (0, 1, rows + 2, rows + 3)
+    totals = [[jnp.zeros((pairs, LANES), F32) for h in range(packs)] for f in range(2)]
 
     def first(pieces):
-        evens, odds = products(wide_one, w_one, mixed_one, [(f, r + 1, count) for f, r, count in pieces])
+        return products(wide_one, w_one, mixed_one, [(f, r + 1, count) for f, r, count in pieces])
+
+    def after_first(pieces, out):
+        evens, odds = combine(out)
         at = 0
         for f, r, count in pieces:
             both = []
@@ -174,7 +177,10 @@
             spread(wide_two, f, r + 1, *both)
 
     def second(pieces):
-        evens, odds = products(wide_two, w_two, mixed_two, pieces)
+        return products(wide_two, w_two, mixed_two, pieces)
+
+    def after_second(pieces, out):
+        evens, odds = combine(out)
         at = 0
         for f, r, count in pieces:
             for first, out in enumerate((evens, odds)):
@@ -188,12 +194,30 @@
                         totals[f][h] = totals[f][h] + value
             at += count * pairs
 
-    totals = [[jnp.zeros((pairs, LANES), F32) for h in range(packs)] for f in range(2)]
-    first([(0, 1, rows - 2)])
-    widen(wide_one, raw, 1, range(2, rows + 2))
-    first([(1, 1, rows - 2)])
-
+    loads[0].wait()
+    stage(raw, 0, 2, maps[0])
+    loads[1].wait()
     pl.semaphore_wait(barrier, devices - 1)
+
+    @pl.when(s < strips - 1)
+    def _():
+        down.start()
+
+    @pl.when(s > 0)
+    def _():
+        up.start()
+
+    widen(wide_one, raw, 0, inner)
+    loads[2].wait()
+    mix(mixed_one, w_one)
+    work = [
+        [(0, 1, rows - 2)],
+        [(0, -1, 2), (0, rows - 1, 2), (1, -1, rows // 2)],
+        [(1, rows // 2 - 1, rows + 2 - rows // 2)],
+    ]
+    done_0 = first(work[0])
+    stage(raw, 1, 2, maps[1])
+    widen(wide_one, raw, 1, inner)
     loads[6].wait()
     told = jnp.full(mark.shape, index[0].astype(F32))
     mark[...] = told
@@ -225,19 +249,6 @@
 
     @pl.when(s < strips - 1)
     def _():
-        down.start()
-
-    @pl.when(s > 0)
-    def _():
-        up.start()
-
-    loads[3].wait()
-    mix(mixed_two, w_two)
-    second([(0, 2, rows - 4)])
-    second([(1, 2, rows - 4)])
-
-    @pl.when(s < strips - 1)
-    def _():
         down.wait_send()
         up.wait_recv()
 
@@ -246,35 +257,47 @@
         up.wait_send()
         down.wait_recv()
 
+    loads[3].wait()
     for f in range(2):
         stage(raw, f, 0, halo[0, f])
         stage(raw, f, rows + 2, halo[1, f])
-        widen(wide_one, raw, f, (0, 1, rows + 2, rows + 3))
-    edges = [(f, r) for f in range(2) for r in (0, rows)]
-    first([(f, r - 1, 2) for f, r in edges])
-    second([(f, min(r, rows - 2), 2) for f, r in edges])
+        widen(wide_one, raw, f, outer)
+    done_1 = first(work[1])
+    after_first(work[0], done_0)
+    mix(mixed_two, w_two)
+    done_2 = first(work[2])
+    after_first(work[1], done_1)
+    frames = [[(f, 0, rows)] for f in range(2)]
+    out_0 = second(frames[0])
+    after_first(work[2], done_2)
+    out_1 = second(frames[1])
+    after_second(frames[0], out_0)
+    after_second(frames[1], out_1)
     cells = rows * strips * columns
     lines = [jnp.sum(total, axis=0, keepdims=True) / cells for frame in totals for total in frame]
     share = jnp.concatenate(lines, axis=0)
     part[...] = share
     parts[me] = share
-    high = 2 * me // devices
-    stride = devices - 1 - (devices - 2) * high
-    nearest = (devices - 1) * (1 - high)
-
-    def send(k, carry):
-        other = lax.rem(nearest + k * stride, devices)
-
-        @pl.when(other != me)
+
+    def send(other, t):
+        pltpu.make_async_remote_copy(
+            src_ref=part, dst_ref=parts.at[me], send_sem=part_send, recv_sem=part_recv,
+            device_id=(other, t), device_id_type=MESH,
+        ).start()
+
+    def spray(k, carry):
+        other = lax.rem(first_peer + k * way, batches)
+
+        @pl.when(other != b)
         def _():
-            pltpu.make_async_remote_copy(
-                src_ref=part, dst_ref=parts.at[me], send_sem=part_send, recv_sem=part_recv,
-                device_id=(other // strips, lax.rem(other, strips)), device_id_type=MESH,
-            ).start()
+            for t in range(strips):
+                send(other, t)
 
         return carry
 
-    lax.fori_loop(0, devices, send, 0)
+    lax.fori_loop(0, batches, spray, 0)
+    for t in range(1, strips):
+        send(b, lax.rem(s + t, strips))
     for i in (4, 5, 7):
         loads[i].wait()
     settle(marks, mark_recv, batches - 1)

time: 20 us -> 19.3 us (0.965)
  Pallas kernels: 17.9 us -> 17.2 us
    pallas_call x1, Pallas kernels: 15.6 us -> 14.8 us  [shards(): pl.pallas_call(functools.partial(block_kernel, batches, strips), out_shap...]
where the time goes in v4:
time: 19.3 us; the launch traced here: 19.2 us
  Pallas kernels  17.2 us (89%)
  between operations  1.93 us (10%)
    pallas_call x1, Pallas kernels, shards(): pl.pallas_call(functools.partial(block_kernel, batches, strips), out_shap...  14.8 us
    pallas_call x1, Pallas kernels, shards(): pl.pallas_call(functools.partial(head_kernel, strips), out_shape=(jax.Sha...  2.4 us

profile of v4, /device:TPU:0, one launch (start us, length us, event | category | flops | bytes accessed | tf_op | source)
XLA Modules:
  0.0 19.2 jit_solution(14379765627671044262)
XLA Ops:
  1.9 14.8 %block.1 = (f32[2,16,2,64,128]{4,3,2,1,0:T(8,128)S(1)}, f32[32,4,128]{2,1,0:T(4,128)S(1)}, f32[17,1,128]{2,1,0:T(1,128)S(1)}, bf16[256,1024]{1,0:T(8,128)(2,1)S(1)}, bf16[256,1024]{1,0:T(8,128)(2,1)S(1)}) custom-call(bf16[1,16,64,256]{3,2,1,0:T(8,128)(2,1)} %state_ref.1, bf16[1,16,64,256]{3,2,1,0:T(8,128)(2,1)} %goal_ref.1, bf16[2304,256]{1,0:T(8,128)(2,1)} %bitcast.2, ...), custom_call_target="tpu_custom_call" | custom-call | tf_op jit(solution)/shard_map/block/pallas_call | solution.py:397
  16.8 2.4 %head.1 = (f32[1]{0:T(128)}, f32[256,1024]{1,0:T(8,128)}, f32[256,1024]{1,0:T(8,128)}, f32[2,1,16,64,256]{4,3,2,1,0:T(8,128)}) custom-call(f32[2,16,2,64,128]{4,3,2,1,0:T(8,128)S(1)} %get-tuple-element.9.block_ref, f32[32,4,128]{2,1,0:T(4,128)S(1)} %get-tuple-element.10.gathered_ref, f32[17,1,128]{2,1,0:T(1,128)S(1)} %get-tuple-element.11.marks_ref, ...), custom_call_target="tpu_custom_call" | custom-call | tf_op jit(solution)/shard_map/head/pallas_call | solution.py:432

commit v5 on v4

--- a/solution.py
+++ b/solution.py
@@ -89,9 +89,9 @@
 def block_kernel(
     batches, strips,
     state_ref, goal_ref, one_ref, two_ref, sproj_ref, gproj_ref, index_ref, temp_ref,
-    block_ref, gathered_ref, marks_out, sproj_out, gproj_out,
-    maps, raw, wide_one, wide_two, w_one, w_two, mixed_one, mixed_two, halo, index, temp, mark, marks, part, parts,
-    load_sem, halo_send, halo_recv, mark_send, mark_recv, part_send, part_recv,
+    block_ref, gathered_ref, temp_out, sproj_out, gproj_out,
+    maps, raw, wide_one, wide_two, w_one, w_two, mixed_one, mixed_two, halo, index, temp, part, parts,
+    load_sem, halo_send, halo_recv, part_send, part_recv,
 ):
     b = lax.axis_index("batch")
     s = lax.axis_index("strip")
@@ -151,6 +151,10 @@
         device_id=(b, lax.rem(s + strips - 1, strips)), device_id_type=MESH,
     )
 
+    def settle(buffer, sem, count):
+        if count:
+            pltpu.make_async_copy(buffer.at[0:count], buffer.at[0:count], sem).wait()
+
     above = jnp.where(s > 0, 1.0, 0.0)
     below = jnp.where(s < strips - 1, 1.0, 0.0)
     pairs = columns // 2
@@ -218,34 +222,6 @@
     done_0 = first(work[0])
     stage(raw, 1, 2, maps[1])
     widen(wide_one, raw, 1, inner)
-    loads[6].wait()
-    told = jnp.full(mark.shape, index[0].astype(F32))
-    mark[...] = told
-    marks[b] = told
-    own = 2 * b // batches
-    way = batches - 1 - (batches - 2) * own
-    first_peer = (batches - 1) * (1 - own)
-
-    def peers(make):
-        def one(k, carry):
-            other = lax.rem(first_peer + k * way, batches)
-
-            @pl.when(other != b)
-            def _():
-                make(other).start()
-
-            return carry
-
-        lax.fori_loop(0, batches, one, 0)
-
-    def settle(buffer, sem, count):
-        if count:
-            pltpu.make_async_copy(buffer.at[0:count], buffer.at[0:count], sem).wait()
-
-    peers(lambda other: pltpu.make_async_remote_copy(
-        src_ref=mark, dst_ref=marks.at[b], send_sem=mark_send, recv_sem=mark_recv,
-        device_id=(other, s), device_id_type=MESH,
-    ))
 
     @pl.when(s < strips - 1)
     def _():
@@ -267,43 +243,43 @@
     mix(mixed_two, w_two)
     done_2 = first(work[2])
     after_first(work[1], done_1)
-    frames = [[(f, 0, rows)] for f in range(2)]
-    out_0 = second(frames[0])
+    half = rows // 2
+    steps = [[(f, r, count)] for f in range(2) for r, count in ((0, half), (half, rows - half))]
+    out = second(steps[0])
     after_first(work[2], done_2)
-    out_1 = second(frames[1])
-    after_second(frames[0], out_0)
-    after_second(frames[1], out_1)
+    for step, later in zip(steps, steps[1:]):
+        following = second(later)
+        after_second(step, out)
+        out = following
+    after_second(steps[-1], out)
     cells = rows * strips * columns
     lines = [jnp.sum(total, axis=0, keepdims=True) / cells for frame in totals for total in frame]
-    share = jnp.concatenate(lines, axis=0)
+    loads[6].wait()
+    lines.append(jnp.full((1, LANES), index[0].astype(F32)))
+    lines.append(jnp.zeros((part.shape[0] - len(lines), LANES), F32))
+    share = jnp.concatenate(lines, axis=0).astype(BF)
     part[...] = share
     parts[me] = share
-
-    def send(other, t):
-        pltpu.make_async_remote_copy(
-            src_ref=part, dst_ref=parts.at[me], send_sem=part_send, recv_sem=part_recv,
-            device_id=(other, t), device_id_type=MESH,
-        ).start()
-
-    def spray(k, carry):
-        other = lax.rem(first_peer + k * way, batches)
-
-        @pl.when(other != b)
+    high = 2 * me // devices
+    stride = devices - 1 - (devices - 2) * high
+    nearest = (devices - 1) * (1 - high)
+
+    def send(k, carry):
+        other = lax.rem(nearest + k * stride, devices)
+
+        @pl.when(other != me)
         def _():
-            for t in range(strips):
-                send(other, t)
+            pltpu.make_async_remote_copy(
+                src_ref=part, dst_ref=parts.at[me], send_sem=part_send, recv_sem=part_recv,
+                device_id=(other // strips, lax.rem(other, strips)), device_id_type=MESH,
+            ).start()
 
         return carry
 
-    lax.fori_loop(0, batches, spray, 0)
-    for t in range(1, strips):
-        send(b, lax.rem(s + t, strips))
+    lax.fori_loop(0, devices, send, 0)
     for i in (4, 5, 7):
         loads[i].wait()
-    settle(marks, mark_recv, batches - 1)
-    settle(marks, mark_send, batches - 1)
-    marks_out[0:batches] = marks[...]
-    marks_out[batches] = jnp.full(mark.shape, temp[0])
+    temp_out[...] = jnp.full(temp_out.shape, temp[0])
     settle(parts, part_recv, devices - 1)
     gathered_ref[...] = parts[...]
     settle(parts, part_send, devices - 1)
@@ -319,7 +295,7 @@
 
 
 def head_kernel(
-    strips, block_ref, gathered_ref, marks_ref, sproj_ref, gproj_ref,
+    strips, block_ref, gathered_ref, temp_ref, sproj_ref, gproj_ref,
     loss_ref, sgrad_ref, ggrad_ref, out_ref,
     loss, sgrad, ggrad, sem,
 ):
@@ -333,7 +309,7 @@
         copy.start()
     batches = gathered_ref.shape[0] // strips
     packs = sproj_ref.shape[0] // LANES
-    told = gathered_ref[...].reshape((batches, strips) + gathered_ref.shape[1:])
+    told = gathered_ref[...].astype(F32).reshape((batches, strips) + gathered_ref.shape[1:])
     heard = told[:, 0]
     for i in range(1, strips):
         heard = heard + told[:, i]
@@ -344,8 +320,8 @@
 
     state_pool = jnp.concatenate([column(p) for p in range(packs)], axis=1).astype(BF)
     goal_pool = jnp.concatenate([column(packs + p) for p in range(packs)], axis=1).astype(BF)
-    index = jnp.concatenate([marks_ref[i] for i in range(batches)], axis=0)[:, 0:1]
-    sharpness = marks_ref[batches][:, 0:1]
+    index = jnp.concatenate([told[i, 0, 2 * packs : 2 * packs + 1] for i in range(batches)], axis=0)[:, 0:1]
+    sharpness = temp_ref[0:1, 0:1]
     state_unit, state_inverse = unit_of(dot(state_pool, sproj_ref[...], (1, 0)))
     goal_unit, goal_inverse = unit_of(dot(goal_pool, gproj_ref[...], (1, 0)))
     state_bf = state_unit.astype(BF)
@@ -385,7 +361,7 @@
     vmem = pl.BlockSpec(memory_space=pltpu.VMEM)
     packs = channels // LANES
     dma = pltpu.SemaphoreType.DMA
-    lines = 2 * packs
+    lines = 8 * pl.cdiv(2 * packs + 1, 8)
     stay = [
         pltpu.with_memory_space_constraint(value, pltpu.HBM)
         for value in (
@@ -398,8 +374,8 @@
         functools.partial(block_kernel, batches, strips),
         out_shape=(
             pltpu.VMEM((2, rows, packs, columns, LANES), F32),
-            pltpu.VMEM((batches * strips, lines, LANES), F32),
-            pltpu.VMEM((batches + 1, 1, LANES), F32),
+            pltpu.VMEM((batches * strips, lines, LANES), BF),
+            pltpu.VMEM((8, LANES), F32),
             pltpu.VMEM((channels, width), BF),
             pltpu.VMEM((channels, width), BF),
         ),
@@ -417,11 +393,9 @@
             pltpu.VMEM((2, 2, 2, columns, channels), BF),
             pltpu.SMEM((1,), jnp.int32),
             pltpu.SMEM((1,), F32),
-            pltpu.VMEM((1, LANES), F32),
-            pltpu.VMEM((batches, 1, LANES), F32),
-            pltpu.VMEM((lines, LANES), F32),
-            pltpu.VMEM((batches * strips, lines, LANES), F32),
-            dma((8,)), dma((2,)), dma((2,)), dma(()), dma(()), dma(()), dma(()),
+            pltpu.VMEM((lines, LANES), BF),
+            pltpu.VMEM((batches * strips, lines, LANES), BF),
+            dma((8,)), dma((2,)), dma((2,)), dma(()), dma(()),
         ],
         compiler_params=pltpu.CompilerParams(
             collective_id=0, has_side_effects=True, vmem_limit_bytes=40 * 2**20

time: 19.3 us -> 19.1 us (0.990)
  no operation moved by 1% of the time
where the time goes in v5:
time: 19.1 us; the launch traced here: 19 us
  Pallas kernels  17.1 us (90%)
  between operations  1.93 us (10%)
    pallas_call x1, Pallas kernels, shards(): pl.pallas_call(functools.partial(block_kernel, batches, strips), out_shap...  14.7 us
    pallas_call x1, Pallas kernels, shards(): pl.pallas_call(functools.partial(head_kernel, strips), out_shape=(jax.Sha...  2.4 us

profile of v5, /device:TPU:0, one launch (start us, length us, event | category | flops | bytes accessed | tf_op | source)
XLA Modules:
  0.0 19.0 jit_solution(17786246570223091547)
XLA Ops:
  1.9 14.7 %block.1 = (f32[2,16,2,64,128]{4,3,2,1,0:T(8,128)S(1)}, bf16[32,8,128]{2,1,0:T(8,128)(2,1)S(1)}, f32[8,128]{1,0:T(8,128)S(1)}, bf16[256,1024]{1,0:T(8,128)(2,1)S(1)}, bf16[256,1024]{1,0:T(8,128)(2,1)S(1)}) custom-call(bf16[1,16,64,256]{3,2,1,0:T(8,128)(2,1)} %state_ref.1, bf16[1,16,64,256]{3,2,1,0:T(8,128)(2,1)} %goal_ref.1, bf16[2304,256]{1,0:T(8,128)(2,1)} %bitcast.2, ...), custom_call_target="tpu_custom_call" | custom-call | tf_op jit(solution)/shard_map/block/pallas_call | solution.py:373
  16.6 2.4 %head.1 = (f32[1]{0:T(128)}, f32[256,1024]{1,0:T(8,128)}, f32[256,1024]{1,0:T(8,128)}, f32[2,1,16,64,256]{4,3,2,1,0:T(8,128)}) custom-call(f32[2,16,2,64,128]{4,3,2,1,0:T(8,128)S(1)} %get-tuple-element.9.block_ref, bf16[32,8,128]{2,1,0:T(8,128)(2,1)S(1)} %get-tuple-element.10.gathered_ref, f32[8,128]{1,0:T(8,128)S(1)} %get-tuple-element.11.temp_ref, ...), custom_call_target="tpu_custom_call" | custom-call | tf_op jit(solution)/shard_map/head/pallas_call | solution.py:406

commit v6 on v5

--- a/solution.py
+++ b/solution.py
@@ -260,23 +260,29 @@
     share = jnp.concatenate(lines, axis=0).astype(BF)
     part[...] = share
     parts[me] = share
-    high = 2 * me // devices
-    stride = devices - 1 - (devices - 2) * high
-    nearest = (devices - 1) * (1 - high)
-
-    def send(k, carry):
-        other = lax.rem(nearest + k * stride, devices)
-
-        @pl.when(other != me)
+    high = 2 * b // batches
+    way = batches - 1 - (batches - 2) * high
+    first_peer = (batches - 1) * (1 - high)
+
+    def send(other, t):
+        pltpu.make_async_remote_copy(
+            src_ref=part, dst_ref=parts.at[me], send_sem=part_send, recv_sem=part_recv,
+            device_id=(other, t), device_id_type=MESH,
+        ).start()
+
+    def spray(k, carry):
+        other = lax.rem(first_peer + k * way, batches)
+
+        @pl.when(other != b)
         def _():
-            pltpu.make_async_remote_copy(
-                src_ref=part, dst_ref=parts.at[me], send_sem=part_send, recv_sem=part_recv,
-                device_id=(other // strips, lax.rem(other, strips)), device_id_type=MESH,
-            ).start()
+            for t in range(strips):
+                send(other, t)
 
         return carry
 
-    lax.fori_loop(0, devices, send, 0)
+    lax.fori_loop(0, batches, spray, 0)
+    for t in range(1, strips):
+        send(b, lax.rem(s + t, strips))
     for i in (4, 5, 7):
         loads[i].wait()
     temp_out[...] = jnp.full(temp_out.shape, temp[0])

time: 19.1 us -> 19.1 us (level)
  no operation moved by 1% of the time
where the time goes in v6:
time: 19.1 us; the launch traced here: 19 us
  Pallas kernels  17 us (89%)
  between operations  1.93 us (10%)
    pallas_call x1, Pallas kernels, shards(): pl.pallas_call(functools.partial(block_kernel, batches, strips), out_shap...  14.6 us
    pallas_call x1, Pallas kernels, shards(): pl.pallas_call(functools.partial(head_kernel, strips), out_shape=(jax.Sha...  2.4 us

profile of v6, /device:TPU:0, one launch (start us, length us, event | category | flops | bytes accessed | tf_op | source)
XLA Modules:
  0.0 19.0 jit_solution(11834069951194456596)
XLA Ops:
  1.9 14.6 %block.1 = (f32[2,16,2,64,128]{4,3,2,1,0:T(8,128)S(1)}, bf16[32,8,128]{2,1,0:T(8,128)(2,1)S(1)}, f32[8,128]{1,0:T(8,128)S(1)}, bf16[256,1024]{1,0:T(8,128)(2,1)S(1)}, bf16[256,1024]{1,0:T(8,128)(2,1)S(1)}) custom-call(bf16[1,16,64,256]{3,2,1,0:T(8,128)(2,1)} %state_ref.1, bf16[1,16,64,256]{3,2,1,0:T(8,128)(2,1)} %goal_ref.1, bf16[2304,256]{1,0:T(8,128)(2,1)} %bitcast.2, ...), custom_call_target="tpu_custom_call" | custom-call | tf_op jit(solution)/shard_map/block/pallas_call | solution.py:379
  16.6 2.4 %head.1 = (f32[1]{0:T(128)}, f32[256,1024]{1,0:T(8,128)}, f32[256,1024]{1,0:T(8,128)}, f32[2,1,16,64,256]{4,3,2,1,0:T(8,128)}) custom-call(f32[2,16,2,64,128]{4,3,2,1,0:T(8,128)S(1)} %get-tuple-element.9.block_ref, bf16[32,8,128]{2,1,0:T(8,128)(2,1)S(1)} %get-tuple-element.10.gathered_ref, f32[8,128]{1,0:T(8,128)S(1)} %get-tuple-element.11.temp_ref, ...), custom_call_target="tpu_custom_call" | custom-call | tf_op jit(solution)/shard_map/head/pallas_call | solution.py:412
